TPU v7x, 32 devices: a whole 2x2x4 slice. The times are simulated.
32 devices in a mesh: grp: 8 (over z, x), dom: 4 (over y, core).
Axes of the slice: x: 2, y: 2, z: 4, core: 2. Of those that a mesh axis runs over, the one named last changes fastest.
Arguments:
- positions: float32 [3, 4096, 512], P(None, ('grp', 'dom')), may hold values from 0 to 1
- velocities: float32 [3, 4096, 512], P(None, ('grp', 'dom')), may hold values from -6 to 6
- masses: float32 [4096, 512], P(('grp', 'dom')), may hold values from 0.5 to 2
- block_halo: int32 [4096], P(('grp', 'dom')), may hold values from 0 to 4095, as said below
- block_shift: int32 [3, 4096], P(None, ('grp', 'dom')), may hold values from -1 to 1
- block_live: int32 [4096], P(('grp', 'dom')), may hold values from 64 to 512
- block_count: int32 [32], P(('grp', 'dom')), may hold values from 32 to 128
- home_slot: int32 [4096], replicated, may hold values from 0 to 4095, as said below
Outputs:
- halo_table: float32 [11, 4096], P(None, ('grp', 'dom'))
- kinetic: float32 [4096, 512], P(('grp', 'dom'))
- radial: float32 [4096, 512], P(('grp', 'dom'))
Inputs may be any that keep to these rules, and one draw needn't show every extreme that they name: A permutation: the halo h is owned by the device of index home_slot[h] // 128 (grp+dom order), in its column home_slot[h] % 128. `block_halo`: the owner of a block's halo lies in the block's own index of grp or in the next one (index + 1, wrapping around); both occur.
All inputs are finite; a program needn't handle non-finite values.
Results may differ from a plain program's by a relative error of at most 0.0003.
Values sent between devices are 32-bit elements; how exact they have to be, the bound alone decides.
A program may use at most 64 MiB of HBM per device.

v0:
```python
import functools

import jax
import jax.numpy as jnp
from jax import lax
from jax.experimental import pallas as pl
from jax.experimental.pallas import tpu as pltpu
from jax.sharding import PartitionSpec as P

BOX = 1.0
EPSILON = 1e-06
MESH = pl.DeviceIdType.MESH
F32 = jnp.float32
BF16 = jnp.bfloat16
LANES = 128
CHUNKS = 2
MASS_ROW = 11


def pieces(x):
    hi = x.astype(BF16).astype(F32)
    rest = x - hi
    mid = rest.astype(BF16).astype(F32)
    return hi, mid, rest - mid


def quotient(x, n):
    return x >> (n.bit_length() - 1) if n & (n - 1) == 0 else x // n


def crossed(a, b):
    return (a[1] * b[2] - a[2] * b[1], a[2] * b[0] - a[0] * b[2], a[0] * b[1] - a[1] * b[0])


def exchange_kernel(
    groups, domains, owned,
    pos_hbm, vel_hbm, mass_hbm, halo_hbm, shift_hbm, live_hbm, count_ref, home_hbm,
    pos, vel, means_ref, sums_ref,
    halo_ref, shift_ref, live_ref, home_ref, small_sem, mass, cols, moments, tables, parts_in, own, own_rest, total_out, near_in, ahead_in, behind_in, rest_in, totals_in,
    in_sem, send1, recv1, send1b, recv1b, send_near, recv_near, send_up, recv_up, send_down, recv_down,
    send_rest, recv_rest, send_total, recv_total,
):
    blocks, width = mass.shape
    rows = blocks // CHUNKS
    g = lax.axis_index("grp")
    d = lax.axis_index("dom")

    def peer(dg, dd):
        return {"grp": lax.rem(g + dg % groups, groups), "dom": lax.rem(d + dd % domains, domains)}

    def remote(src, dst, send, recv, dg, dd):
        return pltpu.make_async_remote_copy(
            src_ref=src, dst_ref=dst, send_sem=send, recv_sem=recv,
            device_id=peer(dg, dd), device_id_type=MESH,
        )

    pairs = ((halo_hbm, halo_ref), (live_hbm, live_ref), (shift_hbm, shift_ref), (home_hbm, home_ref))
    smalls = [
        pltpu.make_async_copy(src, dst, small_sem.at[k]) for k, (src, dst) in enumerate(pairs)
    ]
    for copy in smalls:
        copy.start()
    loads = []
    for c in range(CHUNKS):
        part = pl.ds(c * rows, rows)
        group = [
            pltpu.make_async_copy(mass_hbm.at[part], mass.at[part], in_sem.at[3 * c]),
            pltpu.make_async_copy(pos_hbm.at[:, part], pos.at[:, part], in_sem.at[3 * c + 1]),
            pltpu.make_async_copy(vel_hbm.at[:, part], vel.at[:, part], in_sem.at[3 * c + 2]),
        ]
        for n, copy in enumerate(group):
            copy.start(priority=(c + n) % 2)
        loads.append(group)

    partners = {(0, dd) for dd in range(domains)}
    partners |= {(1 % groups, dd) for dd in range(domains)}
    partners |= {(-1 % groups, dd) for dd in range(domains)}
    partners |= {(dg, 0) for dg in range(groups)}
    partners = sorted(partners - {(0, 0)})
    barrier = pltpu.get_barrier_semaphore()
    for dg, dd in partners:
        pl.semaphore_signal(barrier, inc=1, device_id=peer(dg, dd), device_id_type=MESH)

    for copy in smalls:
        copy.wait()

    lane = lax.broadcasted_iota(jnp.int32, (blocks, LANES), 1)
    row = lax.broadcasted_iota(jnp.int32, (blocks, 1), 0)
    packed = jnp.concatenate(
        [
            halo_ref[...].astype(F32),
            live_ref[...].astype(F32),
            shift_ref[...].astype(F32) * BOX,
            jnp.zeros((LANES - 5, blocks), F32),
        ],
        axis=0,
    )
    turned = packed.T
    live_col = jnp.where(row < count_ref[...], turned[:, 1:2], 0.0)
    cols[...] = jnp.where(lane == 1, live_col, turned)

    halo = turned[:, 0:1].astype(jnp.int32)
    home = home_ref[...]
    home_rows = home.shape[0]
    row_pick = lax.broadcasted_iota(jnp.int32, (blocks, home_rows), 1) == quotient(halo, LANES)
    split = jnp.concatenate([(home >> 8).astype(F32), (home & 255).astype(F32)], axis=1)
    picked = jnp.dot(
        row_pick.astype(F32).astype(BF16), split.astype(BF16), preferred_element_type=F32
    )
    value = picked[:, :LANES] * 256.0 + picked[:, LANES:]
    slot = jnp.sum(jnp.where(lane == (halo & (LANES - 1)), value, 0.0), axis=1, keepdims=True)
    slot = slot.astype(jnp.int32)
    owner = quotient(slot, owned)
    owner_grp = quotient(owner, domains)
    turn = owner - owner_grp * domains - d
    turn = jnp.where(turn < 0, turn + domains, turn)
    column = (jnp.where(owner_grp == g, 0, domains) + turn) * owned + slot - owner * owned
    spread_lanes = lax.broadcasted_iota(jnp.int32, (blocks, 2 * domains * owned), 1)
    onehot = (spread_lanes == column).astype(F32).astype(BF16)

    lane8 = lax.broadcasted_iota(jnp.int32, (8, LANES), 1)
    position8 = lax.broadcasted_iota(jnp.int32, (8, width), 1).astype(F32)

    def fold(x):
        parts = [x[:, i * LANES:(i + 1) * LANES] for i in range(width // LANES)]
        return jnp.sum(functools.reduce(lambda a, b: a + b, parts), axis=1, keepdims=True)

    def moment_rows(start):
        at = pl.ds(start, 8)
        col = cols[at]
        w = jnp.where(position8 < col[:, 1:2], mass[at], 0.0)
        u = [pos[k, at] + col[:, 2 + k:3 + k] for k in range(3)]
        v = [vel[k, at] for k in range(3)]
        wv = [w * x for x in v]
        made = [w] + [w * x for x in u] + wv
        made += [wv[0] * v[0] + wv[1] * v[1] + wv[2] * v[2]]
        made += list(crossed(u, wv))
        out = jnp.zeros((8, LANES), F32)
        for k, x in enumerate(made):
            out = jnp.where(lane8 == k, fold(x), out)
        moments[at] = out

    for c in range(CHUNKS):
        for copy in loads[c]:
            copy.wait()

        def step(i, carry, c=c):
            moment_rows(pl.multiple_of(c * rows + i * 8, 8))
            return carry

        lax.fori_loop(0, rows // 8, step, 0, unroll=True)

    by_row = moments[...].T[:16]
    mass_sum = jnp.sum(by_row[0:1], axis=1, keepdims=True)
    stacked = jnp.concatenate(pieces(by_row), axis=0).astype(BF16)
    product = jnp.dot(stacked, onehot, preferred_element_type=F32)
    product = product[:16] + product[16:32] + product[32:48]
    row8 = lax.broadcasted_iota(jnp.int32, (8, owned), 0)
    for dd in range(domains):
        for ahead in range(2):
            k = ahead * domains + dd
            tile = product[:, k * owned:(k + 1) * owned]
            tables[dd, ahead] = tile[:8]
            tables[dd, 2 + ahead] = jnp.where(row8 == MASS_ROW - 8, mass_sum, tile[8:])

    pl.semaphore_wait(barrier, len(partners))

    first, other = {}, {}
    for part, size, copies, send, recv in ((0, 3, first, send1, recv1), (3, 1, other, send1b, recv1b)):
        for dd in range(1, domains):
            copies[dd] = remote(
                tables.at[dd, pl.ds(part, size)], parts_in.at[dd, pl.ds(part, size)],
                send.at[dd], recv.at[dd], 0, dd,
            )
            copies[dd].start()
    total_of = [tables[0, q] for q in range(4)]
    for dd in range(1, domains):
        first[dd].wait_recv()
        for q in range(3):
            total_of[q] = total_of[q] + parts_in[dd, q]
    own[...] = jnp.stack(total_of[:2], axis=0)
    total_out[0] = total_of[2][MASS_ROW - 8:MASS_ROW - 7]
    mine, ahead = own.at[0], own.at[1]

    second = []
    for dd in list(range(1, domains)) + [0]:
        second.append(
            remote(ahead, behind_in.at[dd], send_up.at[dd], recv_up.at[dd], 1, -dd)
        )
        second.append(
            remote(mine, ahead_in.at[dd], send_down.at[dd], recv_down.at[dd], -1, -dd)
        )
    for dd in range(1, domains):
        second.append(
            remote(own, near_in.at[dd], send_near.at[dd], recv_near.at[dd], 0, -dd)
        )
    late = []
    for dg in sorted(range(1, groups), key=lambda x: -min(x, groups - x)):
        late.append(
            remote(
                total_out.at[0], totals_in.at[dg],
                send_total.at[dg], recv_total.at[dg], dg, 0,
            )
        )
    for copy in late + second:
        copy.start()
    for dd in range(1, domains):
        other[dd].wait_recv()
        total_of[3] = total_of[3] + parts_in[dd, 3]
    own_rest[...] = total_of[3]
    late.append(remote(own_rest, rest_in, send_rest, recv_rest, 1, 0))
    late[-1].start()
    for copy in second:
        copy.wait_recv()

    here, there = [], []
    for dd in range(domains):
        near = [total_of[0], total_of[1]] if dd == 0 else [near_in[dd, 0], near_in[dd, 1]]
        here.append(near[0] + behind_in[dd])
        there.append(near[1] + ahead_in[dd])
    every = jnp.concatenate(here + there, axis=1)
    stacked = jnp.concatenate(list(pieces(every)) + [jnp.zeros_like(every)], axis=0).astype(BF16)
    gathered = lax.dot_general(
        stacked, onehot, (((1,), (1,)), ((), ())), preferred_element_type=F32
    )
    gathered = gathered[0:8] + gathered[8:16] + gathered[16:24]
    centre, drift, spread = halo_means(gathered)
    shifts = packed[2:5]
    live = jnp.where(
        lax.broadcasted_iota(jnp.int32, (1, blocks), 1) < count_ref[...], packed[1:2], 0.0
    )
    by_block = jnp.concatenate(
        [centre[k] - shifts[k:k + 1] for k in range(3)]
        + drift
        + [1.0 / (3.0 * spread + EPSILON), live, jnp.zeros((LANES - 8, blocks), F32)],
        axis=0,
    )
    means_ref[...] = by_block.T

    for copy in late:
        copy.wait_recv()
    total = total_of[2][MASS_ROW - 8:MASS_ROW - 7]
    for dg in range(1, groups):
        total = total + totals_in[dg]
    sums_ref[0:8] = here[0]
    sums_ref[8:16] = jnp.where(row8 == MASS_ROW - 8, total, total_of[2] + rest_in[...])

    for copy in list(first.values()) + list(other.values()) + second + late:
        copy.wait_send()


def halo_means(sums):
    scaled = sums[1:8] * (1.0 / jnp.maximum(sums[0:1], 1.0))
    centre = [scaled[k:k + 1] for k in range(3)]
    drift = [scaled[3 + k:4 + k] for k in range(3)]
    spread = scaled[6:7] - (drift[0] * drift[0] + drift[1] * drift[1] + drift[2] * drift[2])
    return centre, drift, spread


def output_kernel(
    halos, pos, vel, means_ref, sums_ref, table_hbm, kin_hbm, rad_hbm, table, kin, rad, sem
):
    blocks, width = kin.shape
    rows = blocks // CHUNKS
    position8 = lax.broadcasted_iota(jnp.int32, (8, width), 1).astype(F32)

    sums = sums_ref[...]
    centre, drift, spread = halo_means(sums)
    heavy_inv = 1.0 / jnp.maximum(sums[0:1], 1.0)
    turned_spin = crossed(centre, drift)
    spin = [sums[8 + k:9 + k] * heavy_inv - turned_spin[k] for k in range(3)]
    share = sums[0:1] * float(halos) / sums[MASS_ROW:MASS_ROW + 1]
    table[...] = jnp.concatenate([share] + centre + drift + [spread] + spin, axis=0)
    stores = [pltpu.make_async_copy(table, table_hbm, sem.at[2 * CHUNKS])]
    stores[0].start()

    def output_rows(start):
        at = pl.ds(start, 8)
        mean = means_ref[at]
        live = position8 < mean[:, 7:8]
        kinetic = 0.0
        radial = 0.0
        for k in range(3):
            distance = pos[k, at] - mean[:, k:k + 1]
            radial = radial + distance * distance
            offset = vel[k, at] - mean[:, 3 + k:4 + k]
            kinetic = kinetic + offset * offset
        kin[at] = jnp.where(live, kinetic * mean[:, 6:7], 0.0)
        rad[at] = jnp.where(live, radial, 0.0)

    for c in range(CHUNKS):

        def step(i, carry, c=c):
            output_rows(pl.multiple_of(c * rows + i * 8, 8))
            return carry

        lax.fori_loop(0, rows // 8, step, 0, unroll=True)
        part = pl.ds(c * rows, rows)
        group = [
            pltpu.make_async_copy(kin.at[part], kin_hbm.at[part], sem.at[2 * c]),
            pltpu.make_async_copy(rad.at[part], rad_hbm.at[part], sem.at[2 * c + 1]),
        ]
        for copy in group:
            copy.start()
        stores += group
    for copy in stores:
        copy.wait()


def solution(mesh):
    groups, domains = mesh.shape["grp"], mesh.shape["dom"]

    def local(
        positions, velocities, masses, block_halo, block_shift, block_live, block_count, home_slot
    ):
        blocks, width = masses.shape
        halos = home_slot.shape[0]
        owned = halos // (groups * domains)
        vmem = pl.BlockSpec(memory_space=pltpu.VMEM)
        hbm = pl.BlockSpec(memory_space=pl.ANY)
        dma = pltpu.SemaphoreType.DMA
        pos, vel, means, sums = pl.pallas_call(
            functools.partial(exchange_kernel, groups, domains, owned),
            out_shape=(
                pltpu.VMEM((3, blocks, width), F32),
                pltpu.VMEM((3, blocks, width), F32),
                pltpu.VMEM((blocks, LANES), F32),
                pltpu.VMEM((16, owned), F32),
            ),
            in_specs=[hbm, hbm, hbm, hbm, hbm, hbm, vmem, hbm],
            out_specs=(vmem, vmem, vmem, vmem),
            scratch_shapes=[
                pltpu.VMEM((1, blocks), jnp.int32),
                pltpu.VMEM((3, blocks), jnp.int32),
                pltpu.VMEM((1, blocks), jnp.int32),
                pltpu.VMEM((halos // LANES, LANES), jnp.int32),
                dma((4,)),
                pltpu.VMEM((blocks, width), F32),
                pltpu.VMEM((blocks, LANES), F32),
                pltpu.VMEM((blocks, LANES), F32),
                pltpu.VMEM((domains, 4, 8, owned), F32),
                pltpu.VMEM((domains, 4, 8, owned), F32),
                pltpu.VMEM((2, 8, owned), F32),
                pltpu.VMEM((8, owned), F32),
                pltpu.VMEM((1, 1, owned), F32),
                pltpu.VMEM((domains, 2, 8, owned), F32),
                pltpu.VMEM((domains, 8, owned), F32),
                pltpu.VMEM((domains, 8, owned), F32),
                pltpu.VMEM((8, owned), F32),
                pltpu.VMEM((groups, 1, owned), F32),
                dma((3 * CHUNKS,)),
                dma((domains,)), dma((domains,)),
                dma((domains,)), dma((domains,)),
                dma((domains,)), dma((domains,)),
                dma((domains,)), dma((domains,)),
                dma((domains,)), dma((domains,)),
                dma, dma,
                dma((groups,)), dma((groups,)),
            ],
            compiler_params=pltpu.CompilerParams(collective_id=0, has_side_effects=True),
        )(
            positions, velocities, masses,
            block_halo.reshape(1, blocks), block_shift, block_live.reshape(1, blocks),
            block_count.reshape(1, 1), home_slot.reshape(halos // LANES, LANES),
        )
        return pl.pallas_call(
            functools.partial(output_kernel, halos),
            out_shape=(
                jax.ShapeDtypeStruct((11, owned), F32),
                jax.ShapeDtypeStruct((blocks, width), F32),
                jax.ShapeDtypeStruct((blocks, width), F32),
            ),
            in_specs=[vmem, vmem, vmem, vmem],
            out_specs=(hbm, hbm, hbm),
            scratch_shapes=[
                pltpu.VMEM((11, owned), F32),
                pltpu.VMEM((blocks, width), F32),
                pltpu.VMEM((blocks, width), F32),
                dma((2 * CHUNKS + 1,)),
            ],
        )(*[pltpu.with_memory_space_constraint(x, pltpu.VMEM) for x in (pos, vel, means, sums)])

    return jax.shard_map(
        local,
        mesh=mesh,
        in_specs=(
            P(None, ("grp", "dom"), None),
            P(None, ("grp", "dom"), None),
            P(("grp", "dom"), None),
            P(("grp", "dom")),
            P(None, ("grp", "dom")),
            P(("grp", "dom")),
            P(("grp", "dom")),
            P(),
        ),
        out_specs=(P(None, ("grp", "dom")), P(("grp", "dom"), None), P(("grp", "dom"), None)),
        check_vma=False,
    )
```

profile of v0, /device:TPU:0, one launch (start us, length us, event | category | flops | bytes accessed | tf_op | source)
XLA Modules:
  0.0 17.0 jit_solution(15024334753684994580)
XLA Ops:
  1.3 14.7 %shard_map.103 = (f32[3,128,512]{2,1,0:T(8,128)S(1)}, f32[3,128,512]{2,1,0:T(8,128)S(1)}, f32[128,128]{1,0:T(8,128)S(1)}, f32[16,128]{1,0:T(8,128)S(1)}) custom-call(f32[3,128,512]{2,1,0:T(8,128)} %pos_hbm.1, f32[3,128,512]{2,1,0:T(8,128)} %vel_hbm.1, f32[128,512]{1,0:T(8,128)} %mass_hbm.1, s32[1,128]{1,0:T(1,128)} %bitcast.6, s32[3,128]{1,0:T(4,128)} %shift_hbm.1, ...), custom_call_target="tpu_custom_call" | custom-call | tf_op jit(solution)/shard_map/pallas_call | solution.py:322
  16.0 1.0 %shard_map.104 = (f32[11,128]{1,0:T(8,128)}, f32[128,512]{1,0:T(8,128)}, f32[128,512]{1,0:T(8,128)}) custom-call(f32[3,128,512]{2,1,0:T(8,128)S(1)} %get-tuple-element.7.pos, f32[3,128,512]{2,1,0:T(8,128)S(1)} %get-tuple-element.8.vel, f32[128,128]{1,0:T(8,128)S(1)} %get-tuple-element.9.means_ref, f32[16,128]{1,0:T(8,128)S(1)} %get-tuple-element.10.sums_ref), custom_call_target="tpu_custom_call" | custom-call | tf_op jit(solution)/shard_map/pallas_call | solution.py:366
where the time goes:
time: 17.2 us; the launch traced here: 17 us
  Pallas kernels  15.8 us (92%)
  between operations  1.29 us (8%)
    pallas_call x1, Pallas kernels, local(): pl.pallas_call(functools.partial(exchange_kernel, groups, domains, owned)...  14.7 us
    pallas_call x1, Pallas kernels, local(): pl.pallas_call(functools.partial(output_kernel, halos), out_shape=(jax.Sh...  1.04 us

commit v1 on v0

v1 whole, which is shorter than its diff:
```python
import functools

import jax
import jax.numpy as jnp
from jax import lax
from jax.experimental import pallas as pl
from jax.experimental.pallas import tpu as pltpu
from jax.sharding import PartitionSpec as P

BOX = 1.0
EPSILON = 1e-06
MESH = pl.DeviceIdType.MESH
F32 = jnp.float32
BF16 = jnp.bfloat16
LANES = 128
CHUNKS = 4
SLOT_ROW = 8
SPIN_ROW = 9
USED_ROWS = 12
MASS_ROW = 12


def pieces(x):
    hi = x.astype(BF16).astype(F32)
    rest = x - hi
    mid = rest.astype(BF16).astype(F32)
    return hi, mid, rest - mid


def quotient(x, n):
    return x >> (n.bit_length() - 1) if n & (n - 1) == 0 else x // n


def crossed(a, b):
    return (a[1] * b[2] - a[2] * b[1], a[2] * b[0] - a[0] * b[2], a[0] * b[1] - a[1] * b[0])


def exchange_kernel(
    groups, domains, owned,
    pos_hbm, vel_hbm, mass_hbm, halo_hbm, shift_hbm, live_hbm, count_hbm, home_hbm,
    pos, vel, means_ref, sums_ref,
    halo_ref, shift_ref, live_ref, count_ref, home_ref, mass, cols, slots, moments, tile, mass_row, near_in, far_in,
    small_sem, in_sem, send_near, recv_near, send_far, recv_far,
):
    blocks, width = mass.shape
    rows = blocks // CHUNKS
    g = lax.axis_index("grp")
    d = lax.axis_index("dom")

    def wrapped(x, n):
        return jnp.where(x >= n, x - n, x)

    def peer(dg, dd):
        return {"grp": wrapped(g + dg % groups, groups), "dom": wrapped(d + dd % domains, domains)}

    pairs = (
        (live_hbm, live_ref), (count_hbm, count_ref), (halo_hbm, halo_ref), (home_hbm, home_ref),
        (shift_hbm, shift_ref),
    )
    smalls = [
        pltpu.make_async_copy(src, dst, small_sem.at[k]) for k, (src, dst) in enumerate(pairs)
    ]
    for copy in smalls:
        copy.start()
    loads = []
    for c in range(CHUNKS):
        part = pl.ds(c * rows, rows)
        group = [
            pltpu.make_async_copy(mass_hbm.at[part], mass.at[part], in_sem.at[3 * c]),
            pltpu.make_async_copy(pos_hbm.at[:, part], pos.at[:, part], in_sem.at[3 * c + 1]),
            pltpu.make_async_copy(vel_hbm.at[:, part], vel.at[:, part], in_sem.at[3 * c + 2]),
        ]
        for n, copy in enumerate(group):
            copy.start(priority=(c + n) % 2)
        loads.append(group)

    ahead = [(1, dd) for dd in range(domains)]
    behind = [(groups - 1, dd) for dd in range(domains)]
    inside = [(0, dd) for dd in range(1, domains)]
    far = [(dg, dd) for dg in range(2, groups - 1) for dd in range(domains)]
    near = ahead + behind + inside
    barrier = pltpu.get_barrier_semaphore()
    for dg, dd in near + far:
        pl.semaphore_signal(barrier, inc=1, device_id=peer(dg, dd), device_id_type=MESH)

    for copy in smalls:
        copy.wait()

    lane = lax.broadcasted_iota(jnp.int32, (blocks, LANES), 1)
    row = lax.broadcasted_iota(jnp.int32, (blocks, 1), 0)
    packed = jnp.concatenate(
        [
            halo_ref[...].astype(F32),
            live_ref[...].astype(F32),
            jnp.zeros((LANES - 2, blocks), F32),
        ],
        axis=0,
    )
    turned = packed.T
    cols[...] = jnp.where(row < count_ref[0, 0], turned[:, 1:2], 0.0)

    halo = turned[:, 0:1].astype(jnp.int32)
    home = home_ref[...]
    home_rows = home.shape[0]
    row_pick = lax.broadcasted_iota(jnp.int32, (blocks, home_rows), 1) == quotient(halo, LANES)
    split = jnp.concatenate([(home >> 8).astype(F32), (home & 255).astype(F32)], axis=1)
    picked = jnp.dot(
        row_pick.astype(F32).astype(BF16), split.astype(BF16), preferred_element_type=F32
    )
    value = picked[:, :LANES] * 256.0 + picked[:, LANES:]
    slot = jnp.sum(jnp.where(lane == (halo & (LANES - 1)), value, 0.0), axis=1, keepdims=True)
    slots[...] = jnp.broadcast_to(slot, (blocks, LANES))

    lane8 = lax.broadcasted_iota(jnp.int32, (8, LANES), 1)
    shift = shift_ref[...].astype(F32) * BOX

    def moment_rows(start):
        at = pl.ds(start, 8)
        live = jnp.broadcast_to(cols[at], (8, LANES))
        sums = None
        for t in range(width // LANES):
            span = pl.ds(t * LANES, LANES)
            place = (lane8 + t * LANES).astype(F32)
            w = jnp.where(place < live, mass[at, span], 0.0)
            x = [pos[k, at, span] for k in range(3)]
            v = [vel[k, at, span] for k in range(3)]
            wv = [w * y for y in v]
            made = [w] + [w * y for y in x] + wv
            made += [wv[0] * v[0] + wv[1] * v[1] + wv[2] * v[2]]
            made += list(crossed(x, wv))
            sums = made if sums is None else [a + b for a, b in zip(sums, made)]
        out = jnp.where(lane8 == SLOT_ROW, slots[at], 0.0)
        for k, y in enumerate(sums):
            lane_at = k if k < SLOT_ROW else k + 1
            out = jnp.where(lane8 == lane_at, jnp.sum(y, axis=1, keepdims=True), out)
        moments[at] = out

    for c in range(CHUNKS):
        for copy in loads[c]:
            copy.wait()

        def step(i, carry, c=c):
            moment_rows(pl.multiple_of(c * rows + i * 8, 8))
            return carry

        lax.fori_loop(0, rows // 8, step, 0, unroll=True)

    by_row = moments[...].T[:16]
    blank = jnp.zeros((1, blocks), F32)
    s = [shift[k:k + 1] for k in range(3)]
    v = [by_row[4 + k:5 + k] for k in range(3)]

    def stack(x, first):
        return jnp.concatenate([blank] * first + list(x) + [blank] * (5 - first), axis=0)

    first = by_row[0:8] + stack(s, 1) * by_row[0:1]
    turn = stack((s[1], s[2], s[0]), 1) * stack((v[2], v[0], v[1]), 1)
    turn = turn - stack((s[2], s[0], s[1]), 1) * stack((v[1], v[2], v[0]), 1)
    second = by_row[8:16] + turn
    tile[0:8] = first
    tile[8:16] = second
    mass_row[0] = first[0:1]

    pl.semaphore_wait(barrier, len(near) + len(far))

    def near_copy(k, dg, dd):
        part = pl.ds(0, SLOT_ROW + 1) if dg == groups - 1 else pl.ds(0, USED_ROWS)
        return pltpu.make_async_remote_copy(
            src_ref=tile.at[part], dst_ref=near_in.at[k, part],
            send_sem=send_near.at[k], recv_sem=recv_near.at[k],
            device_id=peer(dg, dd), device_id_type=MESH,
        )

    def far_copy(k, dg, dd):
        return pltpu.make_async_remote_copy(
            src_ref=mass_row.at[0], dst_ref=far_in.at[pl.ds(k, 1)],
            send_sem=send_far.at[k], recv_sem=recv_far.at[k],
            device_id=peer(dg, dd), device_id_type=MESH,
        )

    near_copies = [near_copy(k, *p) for k, p in enumerate(near)]
    far_copies = [far_copy(k, *p) for k, p in enumerate(far)]
    from_behind = range(0, domains)
    from_ahead = range(domains, 2 * domains)
    from_inside = range(2 * domains, len(near))
    for copy in near_copies[:2 * domains] + far_copies + near_copies[2 * domains:]:
        copy.start()

    row8 = lax.broadcasted_iota(jnp.int32, (8, blocks), 0)
    base = ((g * domains + d) * owned).astype(F32)
    mine = lax.broadcasted_iota(jnp.int32, (owned, blocks), 0).astype(F32) + base

    def gather(tiles, own):
        left, right = [], []
        for upper, lower in tiles:
            place = lower[0:1]
            hit = (slots[...] == place).astype(F32)
            if own:
                body = jnp.concatenate([upper, jnp.where(row8 < USED_ROWS - 8, lower, 0.0)], axis=0)
                hit = jnp.concatenate([hit, (mine == place).astype(F32)], axis=0)
                left.append(jnp.concatenate(pieces(body), axis=0))
            else:
                left.append(jnp.concatenate(list(pieces(upper)) + [jnp.zeros_like(upper)], axis=0))
            right.append(hit)
        left = jnp.concatenate(left, axis=1).astype(BF16)
        right = jnp.concatenate(right, axis=1).astype(BF16)
        out = lax.dot_general(left, right, (((1,), (1,)), ((), ())), preferred_element_type=F32)
        n = 16 if own else 8
        return out[0:n] + out[n:2 * n] + out[2 * n:3 * n]

    def inbox(ks):
        for k in ks:
            near_copies[k].wait_recv()
        return [(near_in[k, 0:8], near_in[k, 8:16]) for k in ks]

    total = first[0:1]
    tiles = inbox(from_inside)
    total = functools.reduce(lambda a, b: a + b, [t[0][0:1] for t in tiles], total)
    held = gather([(first, second)] + tiles, True)
    means, sums = held[0:8, :blocks], held[:, blocks:]
    tiles = inbox(from_ahead)
    total = functools.reduce(lambda a, b: a + b, [t[0][0:1] for t in tiles], total)
    means = means + gather(tiles, False)
    for copy in near_copies + far_copies:
        copy.wait_send()
    tiles = inbox(from_behind)
    total = functools.reduce(lambda a, b: a + b, [t[0][0:1] for t in tiles], total)
    held = gather(tiles, True)
    means = means + held[0:8, :blocks]
    sums = sums + held[:, blocks:]

    centre, drift, spread = halo_means(means)
    live = jnp.where(
        lax.broadcasted_iota(jnp.int32, (1, blocks), 1) < count_ref[0, 0],
        live_ref[...].astype(F32), 0.0,
    )
    by_block = jnp.concatenate(
        [centre[k] - s[k] for k in range(3)]
        + drift
        + [1.0 / (3.0 * spread + EPSILON), live, jnp.zeros((LANES - 8, blocks), F32)],
        axis=0,
    )
    means_ref[...] = by_block.T

    for copy in far_copies:
        copy.wait_recv()
    if far_copies:
        total = total + jnp.sum(far_in[...], axis=0, keepdims=True)
    sums_ref[0:8] = sums[0:8]
    sums_ref[8:16] = jnp.where(row8 == MASS_ROW - 8, total, sums[8:16])


def halo_means(sums):
    scaled = sums[1:8] * (1.0 / jnp.maximum(sums[0:1], 1.0))
    centre = [scaled[k:k + 1] for k in range(3)]
    drift = [scaled[3 + k:4 + k] for k in range(3)]
    spread = scaled[6:7] - (drift[0] * drift[0] + drift[1] * drift[1] + drift[2] * drift[2])
    return centre, drift, spread


def output_kernel(
    halos, pos, vel, means_ref, sums_ref, table_hbm, kin_hbm, rad_hbm, table, kin, rad, sem
):
    blocks, width = kin.shape
    rows = blocks // CHUNKS
    position8 = lax.broadcasted_iota(jnp.int32, (8, width), 1).astype(F32)

    sums = sums_ref[...]
    centre, drift, spread = halo_means(sums)
    heavy_inv = 1.0 / jnp.maximum(sums[0:1], 1.0)
    turned_spin = crossed(centre, drift)
    spin = [sums[SPIN_ROW + k:SPIN_ROW + 1 + k] * heavy_inv - turned_spin[k] for k in range(3)]
    total = jnp.sum(sums[MASS_ROW:MASS_ROW + 1], axis=1, keepdims=True)
    share = sums[0:1] * float(halos) / total
    table[...] = jnp.concatenate([share] + centre + drift + [spread] + spin, axis=0)
    stores = [pltpu.make_async_copy(table, table_hbm, sem.at[2 * CHUNKS])]
    stores[0].start()

    def output_rows(start):
        at = pl.ds(start, 8)
        mean = means_ref[at]
        live = position8 < mean[:, 7:8]
        kinetic = 0.0
        radial = 0.0
        for k in range(3):
            distance = pos[k, at] - mean[:, k:k + 1]
            radial = radial + distance * distance
            offset = vel[k, at] - mean[:, 3 + k:4 + k]
            kinetic = kinetic + offset * offset
        kin[at] = jnp.where(live, kinetic * mean[:, 6:7], 0.0)
        rad[at] = jnp.where(live, radial, 0.0)

    for c in range(CHUNKS):

        def step(i, carry, c=c):
            output_rows(pl.multiple_of(c * rows + i * 8, 8))
            return carry

        lax.fori_loop(0, rows // 8, step, 0, unroll=True)
        part = pl.ds(c * rows, rows)
        group = [
            pltpu.make_async_copy(kin.at[part], kin_hbm.at[part], sem.at[2 * c]),
            pltpu.make_async_copy(rad.at[part], rad_hbm.at[part], sem.at[2 * c + 1]),
        ]
        for copy in group:
            copy.start()
        stores += group
    for copy in stores:
        copy.wait()


def solution(mesh):
    groups, domains = mesh.shape["grp"], mesh.shape["dom"]

    def local(
        positions, velocities, masses, block_halo, block_shift, block_live, block_count, home_slot
    ):
        blocks, width = masses.shape
        halos = home_slot.shape[0]
        owned = halos // (groups * domains)
        near = 3 * domains - 1
        far = (groups - 3) * domains
        vmem = pl.BlockSpec(memory_space=pltpu.VMEM)
        hbm = pl.BlockSpec(memory_space=pl.ANY)
        dma = pltpu.SemaphoreType.DMA
        pos, vel, means, sums = pl.pallas_call(
            functools.partial(exchange_kernel, groups, domains, owned),
            out_shape=(
                pltpu.VMEM((3, blocks, width), F32),
                pltpu.VMEM((3, blocks, width), F32),
                pltpu.VMEM((blocks, LANES), F32),
                pltpu.VMEM((16, owned), F32),
            ),
            in_specs=[hbm] * 8,
            out_specs=(vmem, vmem, vmem, vmem),
            scratch_shapes=[
                pltpu.VMEM((1, blocks), jnp.int32),
                pltpu.VMEM((3, blocks), jnp.int32),
                pltpu.VMEM((1, blocks), jnp.int32),
                pltpu.SMEM((1, 1), jnp.int32),
                pltpu.VMEM((halos // LANES, LANES), jnp.int32),
                pltpu.VMEM((blocks, width), F32),
                pltpu.VMEM((blocks, 1), F32),
                pltpu.VMEM((blocks, LANES), F32),
                pltpu.VMEM((blocks, LANES), F32),
                pltpu.VMEM((16, blocks), F32),
                pltpu.VMEM((1, 1, blocks), F32),
                pltpu.VMEM((near, 16, blocks), F32),
                pltpu.VMEM((far, blocks), F32),
                dma((5,)), dma((3 * CHUNKS,)),
                dma((near,)), dma((near,)),
                dma((far,)), dma((far,)),
            ],
            compiler_params=pltpu.CompilerParams(collective_id=0, has_side_effects=True),
        )(
            positions, velocities, masses,
            block_halo.reshape(1, blocks), block_shift, block_live.reshape(1, blocks),
            block_count.reshape(1, 1), home_slot.reshape(halos // LANES, LANES),
        )
        return pl.pallas_call(
            functools.partial(output_kernel, halos),
            out_shape=(
                jax.ShapeDtypeStruct((11, owned), F32),
                jax.ShapeDtypeStruct((blocks, width), F32),
                jax.ShapeDtypeStruct((blocks, width), F32),
            ),
            in_specs=[vmem, vmem, vmem, vmem],
            out_specs=(hbm, hbm, hbm),
            scratch_shapes=[
                pltpu.VMEM((11, owned), F32),
                pltpu.VMEM((blocks, width), F32),
                pltpu.VMEM((blocks, width), F32),
                dma((2 * CHUNKS + 1,)),
            ],
        )(*[pltpu.with_memory_space_constraint(x, pltpu.VMEM) for x in (pos, vel, means, sums)])

    return jax.shard_map(
        local,
        mesh=mesh,
        in_specs=(
            P(None, ("grp", "dom"), None),
            P(None, ("grp", "dom"), None),
            P(("grp", "dom"), None),
            P(("grp", "dom")),
            P(None, ("grp", "dom")),
            P(("grp", "dom")),
            P(("grp", "dom")),
            P(),
        ),
        out_specs=(P(None, ("grp", "dom")), P(("grp", "dom"), None), P(("grp", "dom"), None)),
        check_vma=False,
    )
```

time: 17.2 us -> 14.7 us (0.85)
  Pallas kernels: 15.8 us -> 13.2 us
    pallas_call x1, Pallas kernels: 14.7 us -> 12.2 us  [local(): pl.pallas_call(functools.partial(exchange_kernel, groups, domains, owned)...]
where the time goes in v1:
time: 14.7 us; the launch traced here: 14.5 us
  Pallas kernels  13.2 us (90%)
  between operations  1.29 us (9%)
    pallas_call x1, Pallas kernels, local(): pl.pallas_call(functools.partial(exchange_kernel, groups, domains, owned)...  12.2 us
    pallas_call x1, Pallas kernels, local(): pl.pallas_call(functools.partial(output_kernel, halos), out_shape=(jax.Sh...  1.05 us

profile of v1, /device:TPU:0, one launch (start us, length us, event | category | flops | bytes accessed | tf_op | source)
XLA Modules:
  0.0 14.5 jit_solution(5205143823016118087)
XLA Ops:
  1.3 12.2 %shard_map.103 = (f32[3,128,512]{2,1,0:T(8,128)S(1)}, f32[3,128,512]{2,1,0:T(8,128)S(1)}, f32[128,128]{1,0:T(8,128)S(1)}, f32[16,128]{1,0:T(8,128)S(1)}) custom-call(f32[3,128,512]{2,1,0:T(8,128)} %pos_hbm.1, f32[3,128,512]{2,1,0:T(8,128)} %vel_hbm.1, f32[128,512]{1,0:T(8,128)} %mass_hbm.1, s32[1,128]{1,0:T(1,128)} %bitcast.6, s32[3,128]{1,0:T(4,128)} %shift_hbm.1, ...), custom_call_target="tpu_custom_call" | custom-call | tf_op jit(solution)/shard_map/pallas_call | solution.py:326
  13.5 1.0 %shard_map.104 = (f32[11,128]{1,0:T(8,128)}, f32[128,512]{1,0:T(8,128)}, f32[128,512]{1,0:T(8,128)}) custom-call(f32[3,128,512]{2,1,0:T(8,128)S(1)} %get-tuple-element.7.pos, f32[3,128,512]{2,1,0:T(8,128)S(1)} %get-tuple-element.8.vel, f32[128,128]{1,0:T(8,128)S(1)} %get-tuple-element.9.means_ref, f32[16,128]{1,0:T(8,128)S(1)} %get-tuple-element.10.sums_ref), custom_call_target="tpu_custom_call" | custom-call | tf_op jit(solution)/shard_map/pallas_call | solution.py:360

commit v2 on v1

--- a/solution.py
+++ b/solution.py
@@ -17,6 +17,7 @@
 SLOT_ROW = 8
 SPIN_ROW = 9
 USED_ROWS = 12
+SUMS = 11
 MASS_ROW = 12
 
 
@@ -35,15 +36,24 @@
     return (a[1] * b[2] - a[2] * b[1], a[2] * b[0] - a[0] * b[2], a[0] * b[1] - a[1] * b[0])
 
 
+def chunk_spans(blocks):
+    spans, start = [], 0
+    for part in (2, 4, 8, 8):
+        rows = max(blocks // part, 8)
+        spans.append((start, rows))
+        start += rows
+    return spans
+
+
 def exchange_kernel(
     groups, domains, owned,
-    pos_hbm, vel_hbm, mass_hbm, halo_hbm, shift_hbm, live_hbm, count_hbm, home_hbm,
+    pos_hbm, vel_hbm, mass_hbm, halo_hbm, shift_hbm, live_hbm, count_ref, home_hbm,
     pos, vel, means_ref, sums_ref,
-    halo_ref, shift_ref, live_ref, count_ref, home_ref, mass, cols, slots, moments, tile, mass_row, near_in, far_in,
+    halo_ref, shift_ref, live_ref, home_ref, mass, cols, slots, partial, moments, tile, mass_row, near_in, far_in,
     small_sem, in_sem, send_near, recv_near, send_far, recv_far,
 ):
     blocks, width = mass.shape
-    rows = blocks // CHUNKS
+    spans = chunk_spans(blocks)
     g = lax.axis_index("grp")
     d = lax.axis_index("dom")
 
@@ -54,7 +64,7 @@
         return {"grp": wrapped(g + dg % groups, groups), "dom": wrapped(d + dd % domains, domains)}
 
     pairs = (
-        (live_hbm, live_ref), (count_hbm, count_ref), (halo_hbm, halo_ref), (home_hbm, home_ref),
+        (live_hbm, live_ref), (halo_hbm, halo_ref), (home_hbm, home_ref),
         (shift_hbm, shift_ref),
     )
     smalls = [
@@ -62,25 +72,28 @@
     ]
     for copy in smalls:
         copy.start()
+    ahead = [(1, dd) for dd in range(domains)]
+    behind = [(groups - 1, dd) for dd in range(domains)]
+    inside = [(0, dd) for dd in range(1, domains)]
+    far = [(dg, dd) for dg in range(2, groups - 1) for dd in range(domains)]
+    near = ahead + behind + inside
+    barrier = pltpu.get_barrier_semaphore()
+    peers = near + far
+    for dg, dd in peers[:1]:
+        pl.semaphore_signal(barrier, inc=1, device_id=peer(dg, dd), device_id_type=MESH)
     loads = []
-    for c in range(CHUNKS):
-        part = pl.ds(c * rows, rows)
+    for c, (start, rows) in enumerate(spans):
+        part = pl.ds(start, rows)
         group = [
             pltpu.make_async_copy(mass_hbm.at[part], mass.at[part], in_sem.at[3 * c]),
             pltpu.make_async_copy(pos_hbm.at[:, part], pos.at[:, part], in_sem.at[3 * c + 1]),
             pltpu.make_async_copy(vel_hbm.at[:, part], vel.at[:, part], in_sem.at[3 * c + 2]),
         ]
         for n, copy in enumerate(group):
-            copy.start(priority=(c + n) % 2)
+            copy.start(priority=1)
         loads.append(group)
 
-    ahead = [(1, dd) for dd in range(domains)]
-    behind = [(groups - 1, dd) for dd in range(domains)]
-    inside = [(0, dd) for dd in range(1, domains)]
-    far = [(dg, dd) for dg in range(2, groups - 1) for dd in range(domains)]
-    near = ahead + behind + inside
-    barrier = pltpu.get_barrier_semaphore()
-    for dg, dd in near + far:
+    for dg, dd in peers[1:]:
         pl.semaphore_signal(barrier, inc=1, device_id=peer(dg, dd), device_id_type=MESH)
 
     for copy in smalls:
@@ -92,12 +105,13 @@
         [
             halo_ref[...].astype(F32),
             live_ref[...].astype(F32),
-            jnp.zeros((LANES - 2, blocks), F32),
+            jnp.zeros((6, blocks), F32),
         ],
         axis=0,
     )
     turned = packed.T
-    cols[...] = jnp.where(row < count_ref[0, 0], turned[:, 1:2], 0.0)
+    live_col = jnp.where(row < count_ref[0], turned[:, 1:2], 0.0)
+    cols[...] = jnp.broadcast_to(live_col, (blocks, LANES))
 
     halo = turned[:, 0:1].astype(jnp.int32)
     home = home_ref[...]
@@ -114,9 +128,9 @@
     lane8 = lax.broadcasted_iota(jnp.int32, (8, LANES), 1)
     shift = shift_ref[...].astype(F32) * BOX
 
-    def moment_rows(start):
+    def add_up(start):
         at = pl.ds(start, 8)
-        live = jnp.broadcast_to(cols[at], (8, LANES))
+        live = cols[at]
         sums = None
         for t in range(width // LANES):
             span = pl.ds(t * LANES, LANES)
@@ -129,21 +143,28 @@
             made += [wv[0] * v[0] + wv[1] * v[1] + wv[2] * v[2]]
             made += list(crossed(x, wv))
             sums = made if sums is None else [a + b for a, b in zip(sums, made)]
+        for k, y in enumerate(sums):
+            partial[k, at] = y
+
+    def fold(start):
+        at = pl.ds(start, 8)
         out = jnp.where(lane8 == SLOT_ROW, slots[at], 0.0)
-        for k, y in enumerate(sums):
+        for k in range(SUMS):
             lane_at = k if k < SLOT_ROW else k + 1
-            out = jnp.where(lane8 == lane_at, jnp.sum(y, axis=1, keepdims=True), out)
+            out = jnp.where(lane8 == lane_at, jnp.sum(partial[k, at], axis=1, keepdims=True), out)
         moments[at] = out
 
-    for c in range(CHUNKS):
+    done = []
+    for c, (start, rows) in enumerate(spans):
         for copy in loads[c]:
             copy.wait()
-
-        def step(i, carry, c=c):
-            moment_rows(pl.multiple_of(c * rows + i * 8, 8))
-            return carry
-
-        lax.fori_loop(0, rows // 8, step, 0, unroll=True)
+        for i in range(start, start + rows, 8):
+            add_up(i)
+        for i in done:
+            fold(i)
+        done = range(start, start + rows, 8)
+    for i in done:
+        fold(i)
 
     by_row = moments[...].T[:16]
     blank = jnp.zeros((1, blocks), F32)
@@ -231,7 +252,7 @@
 
     centre, drift, spread = halo_means(means)
     live = jnp.where(
-        lax.broadcasted_iota(jnp.int32, (1, blocks), 1) < count_ref[0, 0],
+        lax.broadcasted_iota(jnp.int32, (1, blocks), 1) < count_ref[0],
         live_ref[...].astype(F32), 0.0,
     )
     by_block = jnp.concatenate(
@@ -331,23 +352,23 @@
                 pltpu.VMEM((blocks, LANES), F32),
                 pltpu.VMEM((16, owned), F32),
             ),
-            in_specs=[hbm] * 8,
+            in_specs=[hbm] * 6 + [pl.BlockSpec(memory_space=pltpu.SMEM), hbm],
             out_specs=(vmem, vmem, vmem, vmem),
             scratch_shapes=[
                 pltpu.VMEM((1, blocks), jnp.int32),
                 pltpu.VMEM((3, blocks), jnp.int32),
                 pltpu.VMEM((1, blocks), jnp.int32),
-                pltpu.SMEM((1, 1), jnp.int32),
                 pltpu.VMEM((halos // LANES, LANES), jnp.int32),
                 pltpu.VMEM((blocks, width), F32),
-                pltpu.VMEM((blocks, 1), F32),
                 pltpu.VMEM((blocks, LANES), F32),
+                pltpu.VMEM((blocks, LANES), F32),
+                pltpu.VMEM((SUMS, blocks, LANES), F32),
                 pltpu.VMEM((blocks, LANES), F32),
                 pltpu.VMEM((16, blocks), F32),
                 pltpu.VMEM((1, 1, blocks), F32),
                 pltpu.VMEM((near, 16, blocks), F32),
                 pltpu.VMEM((far, blocks), F32),
-                dma((5,)), dma((3 * CHUNKS,)),
+                dma((4,)), dma((3 * len(chunk_spans(blocks)),)),
                 dma((near,)), dma((near,)),
                 dma((far,)), dma((far,)),
             ],
@@ -355,7 +376,7 @@
         )(
             positions, velocities, masses,
             block_halo.reshape(1, blocks), block_shift, block_live.reshape(1, blocks),
-            block_count.reshape(1, 1), home_slot.reshape(halos // LANES, LANES),
+            block_count, home_slot.reshape(halos // LANES, LANES),
         )
         return pl.pallas_call(
             functools.partial(output_kernel, halos),

time: 14.7 us -> 14.1 us (0.959)
  Pallas kernels: 13.2 us -> 12.7 us
    pallas_call x1, Pallas kernels: 12.2 us -> 11.6 us  [local(): pl.pallas_call(functools.partial(exchange_kernel, groups, domains, owned)...]
where the time goes in v2:
time: 14.1 us; the launch traced here: 13.9 us
  Pallas kernels  12.7 us (90%)
  between operations  1.29 us (9%)
    pallas_call x1, Pallas kernels, local(): pl.pallas_call(functools.partial(exchange_kernel, groups, domains, owned)...  11.6 us
    pallas_call x1, Pallas kernels, local(): pl.pallas_call(functools.partial(output_kernel, halos), out_shape=(jax.Sh...  1.05 us

profile of v2, /device:TPU:0, one launch (start us, length us, event | category | flops | bytes accessed | tf_op | source)
XLA Modules:
  0.0 13.9 jit_solution(8729589798807720609)
XLA Ops:
  1.3 11.6 %shard_map.103 = (f32[3,128,512]{2,1,0:T(8,128)S(1)}, f32[3,128,512]{2,1,0:T(8,128)S(1)}, f32[128,128]{1,0:T(8,128)S(1)}, f32[16,128]{1,0:T(8,128)S(1)}) custom-call(f32[3,128,512]{2,1,0:T(8,128)} %pos_hbm.1, f32[3,128,512]{2,1,0:T(8,128)} %vel_hbm.1, f32[128,512]{1,0:T(8,128)} %mass_hbm.1, s32[1,128]{1,0:T(1,128)} %bitcast.4, s32[3,128]{1,0:T(4,128)} %shift_hbm.1, ...), custom_call_target="tpu_custom_call" | custom-call | tf_op jit(solution)/shard_map/pallas_call | solution.py:347
  12.9 1.0 %shard_map.104 = (f32[11,128]{1,0:T(8,128)}, f32[128,512]{1,0:T(8,128)}, f32[128,512]{1,0:T(8,128)}) custom-call(f32[3,128,512]{2,1,0:T(8,128)S(1)} %get-tuple-element.7.pos, f32[3,128,512]{2,1,0:T(8,128)S(1)} %get-tuple-element.8.vel, f32[128,128]{1,0:T(8,128)S(1)} %get-tuple-element.9.means_ref, f32[16,128]{1,0:T(8,128)S(1)} %get-tuple-element.10.sums_ref), custom_call_target="tpu_custom_call" | custom-call | tf_op jit(solution)/shard_map/pallas_call | solution.py:381

commit v3 on v2

--- a/solution.py
+++ b/solution.py
@@ -37,12 +37,10 @@
 
 
 def chunk_spans(blocks):
-    spans, start = [], 0
-    for part in (2, 4, 8, 8):
-        rows = max(blocks // part, 8)
-        spans.append((start, rows))
-        start += rows
-    return spans
+    tail = max(blocks // 8, 8)
+    middle = max(3 * blocks // 8 // 8 * 8, 8)
+    first = blocks - middle - tail
+    return [(0, first), (first, middle), (first + middle, tail)]
 
 
 def exchange_kernel(
@@ -68,14 +66,15 @@
         (shift_hbm, shift_ref),
     )
     smalls = [
-        pltpu.make_async_copy(src, dst, small_sem.at[k]) for k, (src, dst) in enumerate(pairs)
+        pltpu.make_async_copy(src, dst, small_sem) for src, dst in pairs
     ]
     for copy in smalls:
         copy.start()
-    ahead = [(1, dd) for dd in range(domains)]
-    behind = [(groups - 1, dd) for dd in range(domains)]
-    inside = [(0, dd) for dd in range(1, domains)]
-    far = [(dg, dd) for dg in range(2, groups - 1) for dd in range(domains)]
+    turns = sorted(range(domains), key=lambda dd: -min(dd, domains - dd))
+    ahead = [(1, dd) for dd in turns]
+    behind = [(groups - 1, dd) for dd in turns]
+    inside = [(0, dd) for dd in turns[:-1]]
+    far = [(dg, dd) for dg in range(2, groups - 1) for dd in turns]
     near = ahead + behind + inside
     barrier = pltpu.get_barrier_semaphore()
     peers = near + far
@@ -85,11 +84,11 @@
     for c, (start, rows) in enumerate(spans):
         part = pl.ds(start, rows)
         group = [
-            pltpu.make_async_copy(mass_hbm.at[part], mass.at[part], in_sem.at[3 * c]),
-            pltpu.make_async_copy(pos_hbm.at[:, part], pos.at[:, part], in_sem.at[3 * c + 1]),
-            pltpu.make_async_copy(vel_hbm.at[:, part], vel.at[:, part], in_sem.at[3 * c + 2]),
+            pltpu.make_async_copy(mass_hbm.at[part], mass.at[part], in_sem.at[c]),
+            pltpu.make_async_copy(pos_hbm.at[:, part], pos.at[:, part], in_sem.at[c]),
+            pltpu.make_async_copy(vel_hbm.at[:, part], vel.at[:, part], in_sem.at[c]),
         ]
-        for n, copy in enumerate(group):
+        for copy in group:
             copy.start(priority=1)
         loads.append(group)
 
@@ -184,28 +183,28 @@
 
     pl.semaphore_wait(barrier, len(near) + len(far))
 
-    def near_copy(k, dg, dd):
-        part = pl.ds(0, SLOT_ROW + 1) if dg == groups - 1 else pl.ds(0, USED_ROWS)
+    def remote(src, dst, send, recv, dg, dd):
         return pltpu.make_async_remote_copy(
-            src_ref=tile.at[part], dst_ref=near_in.at[k, part],
-            send_sem=send_near.at[k], recv_sem=recv_near.at[k],
+            src_ref=src, dst_ref=dst, send_sem=send, recv_sem=recv,
             device_id=peer(dg, dd), device_id_type=MESH,
         )
 
-    def far_copy(k, dg, dd):
-        return pltpu.make_async_remote_copy(
-            src_ref=mass_row.at[0], dst_ref=far_in.at[pl.ds(k, 1)],
-            send_sem=send_far.at[k], recv_sem=recv_far.at[k],
-            device_id=peer(dg, dd), device_id_type=MESH,
-        )
-
-    near_copies = [near_copy(k, *p) for k, p in enumerate(near)]
-    far_copies = [far_copy(k, *p) for k, p in enumerate(far)]
-    from_behind = range(0, domains)
-    from_ahead = range(domains, 2 * domains)
-    from_inside = range(2 * domains, len(near))
-    for copy in near_copies[:2 * domains] + far_copies + near_copies[2 * domains:]:
-        copy.start()
+    used = pl.ds(0, USED_ROWS)
+    from_behind, from_ahead, from_inside = 0, 1, 2
+
+    def landing(k):
+        return near_in.at[pl.ds(k * domains, domains if k < from_inside else domains - 1), used]
+
+    for k, (dg, dd) in enumerate(near[:2 * domains]):
+        remote(
+            tile.at[used], near_in.at[k, used], send_near, recv_near.at[k // domains], dg, dd
+        ).start()
+    for k, (dg, dd) in enumerate(far):
+        remote(mass_row.at[0], far_in.at[pl.ds(k, 1)], send_far, recv_far, dg, dd).start()
+    for k, (dg, dd) in enumerate(near[2 * domains:], 2 * domains):
+        remote(
+            tile.at[used], near_in.at[k, used], send_near, recv_near.at[k // domains], dg, dd
+        ).start()
 
     row8 = lax.broadcasted_iota(jnp.int32, (8, blocks), 0)
     base = ((g * domains + d) * owned).astype(F32)
@@ -229,23 +228,29 @@
         n = 16 if own else 8
         return out[0:n] + out[n:2 * n] + out[2 * n:3 * n]
 
-    def inbox(ks):
-        for k in ks:
-            near_copies[k].wait_recv()
-        return [(near_in[k, 0:8], near_in[k, 8:16]) for k in ks]
-
-    total = first[0:1]
+    def inbox(k):
+        whole = landing(k)
+        remote(whole, whole, send_near, recv_near.at[k], *near[0]).wait_recv()
+        at = range(k * domains, (k + 1) * domains if k < from_inside else len(near))
+        return [(near_in[n, 0:8], near_in[n, 8:16]) for n in at]
+
+    def masses_of(tiles):
+        return functools.reduce(lambda a, b: a + b, [t[0][0:1] for t in tiles])
+
     tiles = inbox(from_inside)
-    total = functools.reduce(lambda a, b: a + b, [t[0][0:1] for t in tiles], total)
+    total = first[0:1] + masses_of(tiles)
     held = gather([(first, second)] + tiles, True)
     means, sums = held[0:8, :blocks], held[:, blocks:]
     tiles = inbox(from_ahead)
-    total = functools.reduce(lambda a, b: a + b, [t[0][0:1] for t in tiles], total)
+    total = total + masses_of(tiles)
     means = means + gather(tiles, False)
-    for copy in near_copies + far_copies:
-        copy.wait_send()
+    whole = near_in.at[:, used]
+    remote(whole, whole, send_near, recv_near.at[0], *near[0]).wait_send()
+    if far:
+        remote(far_in, far_in, send_far, recv_far, *near[0]).wait()
+        total = total + jnp.sum(far_in[...], axis=0, keepdims=True)
     tiles = inbox(from_behind)
-    total = functools.reduce(lambda a, b: a + b, [t[0][0:1] for t in tiles], total)
+    total = total + masses_of(tiles)
     held = gather(tiles, True)
     means = means + held[0:8, :blocks]
     sums = sums + held[:, blocks:]
@@ -258,15 +263,10 @@
     by_block = jnp.concatenate(
         [centre[k] - s[k] for k in range(3)]
         + drift
-        + [1.0 / (3.0 * spread + EPSILON), live, jnp.zeros((LANES - 8, blocks), F32)],
+        + [1.0 / (3.0 * spread + EPSILON), live],
         axis=0,
     )
-    means_ref[...] = by_block.T
-
-    for copy in far_copies:
-        copy.wait_recv()
-    if far_copies:
-        total = total + jnp.sum(far_in[...], axis=0, keepdims=True)
+    means_ref[:, 0:8] = by_block.T
     sums_ref[0:8] = sums[0:8]
     sums_ref[8:16] = jnp.where(row8 == MASS_ROW - 8, total, sums[8:16])
 
@@ -294,7 +294,7 @@
     total = jnp.sum(sums[MASS_ROW:MASS_ROW + 1], axis=1, keepdims=True)
     share = sums[0:1] * float(halos) / total
     table[...] = jnp.concatenate([share] + centre + drift + [spread] + spin, axis=0)
-    stores = [pltpu.make_async_copy(table, table_hbm, sem.at[2 * CHUNKS])]
+    stores = [pltpu.make_async_copy(table, table_hbm, sem)]
     stores[0].start()
 
     def output_rows(start):
@@ -320,8 +320,8 @@
         lax.fori_loop(0, rows // 8, step, 0, unroll=True)
         part = pl.ds(c * rows, rows)
         group = [
-            pltpu.make_async_copy(kin.at[part], kin_hbm.at[part], sem.at[2 * c]),
-            pltpu.make_async_copy(rad.at[part], rad_hbm.at[part], sem.at[2 * c + 1]),
+            pltpu.make_async_copy(kin.at[part], kin_hbm.at[part], sem),
+            pltpu.make_async_copy(rad.at[part], rad_hbm.at[part], sem),
         ]
         for copy in group:
             copy.start()
@@ -368,9 +368,9 @@
                 pltpu.VMEM((1, 1, blocks), F32),
                 pltpu.VMEM((near, 16, blocks), F32),
                 pltpu.VMEM((far, blocks), F32),
-                dma((4,)), dma((3 * len(chunk_spans(blocks)),)),
-                dma((near,)), dma((near,)),
-                dma((far,)), dma((far,)),
+                dma, dma((len(chunk_spans(blocks)),)),
+                dma, dma((3,)),
+                dma, dma,
             ],
             compiler_params=pltpu.CompilerParams(collective_id=0, has_side_effects=True),
         )(
@@ -391,7 +391,7 @@
                 pltpu.VMEM((11, owned), F32),
                 pltpu.VMEM((blocks, width), F32),
                 pltpu.VMEM((blocks, width), F32),
-                dma((2 * CHUNKS + 1,)),
+                dma,
             ],
         )(*[pltpu.with_memory_space_constraint(x, pltpu.VMEM) for x in (pos, vel, means, sums)])
 

time: 14.1 us -> 13.3 us (0.943)
  Pallas kernels: 12.7 us -> 11.8 us
    pallas_call x1, Pallas kernels: 11.6 us -> 10.8 us  [local(): pl.pallas_call(functools.partial(exchange_kernel, groups, domains, owned)...]
where the time goes in v3:
time: 13.3 us; the launch traced here: 13.1 us
  Pallas kernels  11.8 us (89%)
  between operations  1.29 us (10%)
    pallas_call x1, Pallas kernels, local(): pl.pallas_call(functools.partial(exchange_kernel, groups, domains, owned)...  10.8 us
    pallas_call x1, Pallas kernels, local(): pl.pallas_call(functools.partial(output_kernel, halos), out_shape=(jax.Sh...  0.98 us

profile of v3, /device:TPU:0, one launch (start us, length us, event | category | flops | bytes accessed | tf_op | source)
XLA Modules:
  0.0 13.1 jit_solution(9058412437557222334)
XLA Ops:
  1.3 10.8 %shard_map.103 = (f32[3,128,512]{2,1,0:T(8,128)S(1)}, f32[3,128,512]{2,1,0:T(8,128)S(1)}, f32[128,128]{1,0:T(8,128)S(1)}, f32[16,128]{1,0:T(8,128)S(1)}) custom-call(f32[3,128,512]{2,1,0:T(8,128)} %pos_hbm.1, f32[3,128,512]{2,1,0:T(8,128)} %vel_hbm.1, f32[128,512]{1,0:T(8,128)} %mass_hbm.1, s32[1,128]{1,0:T(1,128)} %bitcast.4, s32[3,128]{1,0:T(4,128)} %shift_hbm.1, ...), custom_call_target="tpu_custom_call" | custom-call | tf_op jit(solution)/shard_map/pallas_call | solution.py:347
  12.1 1.0 %shard_map.104 = (f32[11,128]{1,0:T(8,128)}, f32[128,512]{1,0:T(8,128)}, f32[128,512]{1,0:T(8,128)}) custom-call(f32[3,128,512]{2,1,0:T(8,128)S(1)} %get-tuple-element.7.pos, f32[3,128,512]{2,1,0:T(8,128)S(1)} %get-tuple-element.8.vel, f32[128,128]{1,0:T(8,128)S(1)} %get-tuple-element.9.means_ref, f32[16,128]{1,0:T(8,128)S(1)} %get-tuple-element.10.sums_ref), custom_call_target="tpu_custom_call" | custom-call | tf_op jit(solution)/shard_map/pallas_call | solution.py:381

commit v4 on v3

--- a/solution.py
+++ b/solution.py
@@ -46,9 +46,9 @@
 def exchange_kernel(
     groups, domains, owned,
     pos_hbm, vel_hbm, mass_hbm, halo_hbm, shift_hbm, live_hbm, count_ref, home_hbm,
-    pos, vel, means_ref, sums_ref,
-    halo_ref, shift_ref, live_ref, home_ref, mass, cols, slots, partial, moments, tile, mass_row, near_in, far_in,
-    small_sem, in_sem, send_near, recv_near, send_far, recv_far,
+    pos, vel, means_ref, sums_ref, cols,
+    halo_ref, shift_ref, live_ref, home_ref, mass, slots, partial, moments, tile, mass_row, near_in, far_in,
+    small_sem, in_sem, recv_sem,
 ):
     blocks, width = mass.shape
     spans = chunk_spans(blocks)
@@ -153,17 +153,12 @@
             out = jnp.where(lane8 == lane_at, jnp.sum(partial[k, at], axis=1, keepdims=True), out)
         moments[at] = out
 
-    done = []
     for c, (start, rows) in enumerate(spans):
         for copy in loads[c]:
             copy.wait()
         for i in range(start, start + rows, 8):
             add_up(i)
-        for i in done:
             fold(i)
-        done = range(start, start + rows, 8)
-    for i in done:
-        fold(i)
 
     by_row = moments[...].T[:16]
     blank = jnp.zeros((1, blocks), F32)
@@ -191,20 +186,18 @@
 
     used = pl.ds(0, USED_ROWS)
     from_behind, from_ahead, from_inside = 0, 1, 2
-
-    def landing(k):
-        return near_in.at[pl.ds(k * domains, domains if k < from_inside else domains - 1), used]
-
-    for k, (dg, dd) in enumerate(near[:2 * domains]):
-        remote(
-            tile.at[used], near_in.at[k, used], send_near, recv_near.at[k // domains], dg, dd
-        ).start()
+    send, send_far = in_sem.at[0], in_sem.at[1]
+    late, early, recv_far = (recv_sem.at[k] for k in range(3))
+
+    def send_near(first, last):
+        for k in range(first, last):
+            recv = late if k < domains else early
+            remote(tile.at[used], near_in.at[k, used], send, recv, *near[k]).start()
+
+    send_near(0, 2 * domains)
     for k, (dg, dd) in enumerate(far):
         remote(mass_row.at[0], far_in.at[pl.ds(k, 1)], send_far, recv_far, dg, dd).start()
-    for k, (dg, dd) in enumerate(near[2 * domains:], 2 * domains):
-        remote(
-            tile.at[used], near_in.at[k, used], send_near, recv_near.at[k // domains], dg, dd
-        ).start()
+    send_near(2 * domains, len(near))
 
     row8 = lax.broadcasted_iota(jnp.int32, (8, blocks), 0)
     base = ((g * domains + d) * owned).astype(F32)
@@ -228,15 +221,19 @@
         n = 16 if own else 8
         return out[0:n] + out[n:2 * n] + out[2 * n:3 * n]
 
+    def landed(ref, recv):
+        remote(ref, ref, send, recv, *near[0]).wait_recv()
+
     def inbox(k):
-        whole = landing(k)
-        remote(whole, whole, send_near, recv_near.at[k], *near[0]).wait_recv()
         at = range(k * domains, (k + 1) * domains if k < from_inside else len(near))
         return [(near_in[n, 0:8], near_in[n, 8:16]) for n in at]
 
     def masses_of(tiles):
         return functools.reduce(lambda a, b: a + b, [t[0][0:1] for t in tiles])
 
+    landed(near_in.at[pl.ds(domains, len(near) - domains), used], early)
+    if far:
+        landed(far_in, recv_far)
     tiles = inbox(from_inside)
     total = first[0:1] + masses_of(tiles)
     held = gather([(first, second)] + tiles, True)
@@ -245,10 +242,11 @@
     total = total + masses_of(tiles)
     means = means + gather(tiles, False)
     whole = near_in.at[:, used]
-    remote(whole, whole, send_near, recv_near.at[0], *near[0]).wait_send()
+    remote(whole, whole, send, early, *near[0]).wait_send()
     if far:
-        remote(far_in, far_in, send_far, recv_far, *near[0]).wait()
+        remote(far_in, far_in, send_far, recv_far, *near[0]).wait_send()
         total = total + jnp.sum(far_in[...], axis=0, keepdims=True)
+    landed(near_in.at[pl.ds(0, domains), used], late)
     tiles = inbox(from_behind)
     total = total + masses_of(tiles)
     held = gather(tiles, True)
@@ -256,14 +254,10 @@
     sums = sums + held[:, blocks:]
 
     centre, drift, spread = halo_means(means)
-    live = jnp.where(
-        lax.broadcasted_iota(jnp.int32, (1, blocks), 1) < count_ref[0],
-        live_ref[...].astype(F32), 0.0,
-    )
     by_block = jnp.concatenate(
         [centre[k] - s[k] for k in range(3)]
         + drift
-        + [1.0 / (3.0 * spread + EPSILON), live],
+        + [1.0 / (3.0 * spread + EPSILON), blank],
         axis=0,
     )
     means_ref[:, 0:8] = by_block.T
@@ -280,36 +274,43 @@
 
 
 def output_kernel(
-    halos, pos, vel, means_ref, sums_ref, table_hbm, kin_hbm, rad_hbm, table, kin, rad, sem
+    halos, pos, vel, means_ref, sums_ref, live_ref, table_hbm, kin_hbm, rad_hbm, table, kin, rad, sem
 ):
     blocks, width = kin.shape
     rows = blocks // CHUNKS
-    position8 = lax.broadcasted_iota(jnp.int32, (8, width), 1).astype(F32)
-
-    sums = sums_ref[...]
-    centre, drift, spread = halo_means(sums)
-    heavy_inv = 1.0 / jnp.maximum(sums[0:1], 1.0)
-    turned_spin = crossed(centre, drift)
-    spin = [sums[SPIN_ROW + k:SPIN_ROW + 1 + k] * heavy_inv - turned_spin[k] for k in range(3)]
-    total = jnp.sum(sums[MASS_ROW:MASS_ROW + 1], axis=1, keepdims=True)
-    share = sums[0:1] * float(halos) / total
-    table[...] = jnp.concatenate([share] + centre + drift + [spread] + spin, axis=0)
-    stores = [pltpu.make_async_copy(table, table_hbm, sem)]
-    stores[0].start()
+    stores = []
+
+    lane8 = lax.broadcasted_iota(jnp.int32, (8, LANES), 1)
 
     def output_rows(start):
         at = pl.ds(start, 8)
         mean = means_ref[at]
-        live = position8 < mean[:, 7:8]
-        kinetic = 0.0
-        radial = 0.0
-        for k in range(3):
-            distance = pos[k, at] - mean[:, k:k + 1]
-            radial = radial + distance * distance
-            offset = vel[k, at] - mean[:, 3 + k:4 + k]
-            kinetic = kinetic + offset * offset
-        kin[at] = jnp.where(live, kinetic * mean[:, 6:7], 0.0)
-        rad[at] = jnp.where(live, radial, 0.0)
+        mean = [jnp.broadcast_to(mean[:, k:k + 1], (8, LANES)) for k in range(7)]
+        live = live_ref[at]
+        for t in range(width // LANES):
+            span = pl.ds(t * LANES, LANES)
+            kinetic, radial = 0.0, 0.0
+            for k in range(3):
+                distance = pos[k, at, span] - mean[k]
+                radial = radial + distance * distance
+                offset = vel[k, at, span] - mean[3 + k]
+                kinetic = kinetic + offset * offset
+            kept = (lane8 + t * LANES).astype(F32) < live
+            kin[at, span] = jnp.where(kept, kinetic * mean[6], 0.0)
+            rad[at, span] = jnp.where(kept, radial, 0.0)
+
+    def make_table():
+        sums = sums_ref[...]
+        centre, drift, spread = halo_means(sums)
+        heavy_inv = 1.0 / jnp.maximum(sums[0:1], 1.0)
+        turned_spin = crossed(centre, drift)
+        spin = [sums[SPIN_ROW + k:SPIN_ROW + 1 + k] * heavy_inv - turned_spin[k] for k in range(3)]
+        total = jnp.sum(sums[MASS_ROW:MASS_ROW + 1], axis=1, keepdims=True)
+        share = sums[0:1] * float(halos) / total
+        table[...] = jnp.concatenate([share] + centre + drift + [spread] + spin, axis=0)
+        copy = pltpu.make_async_copy(table, table_hbm, sem)
+        copy.start()
+        return copy
 
     for c in range(CHUNKS):
 
@@ -326,6 +327,8 @@
         for copy in group:
             copy.start()
         stores += group
+        if c == 1:
+            stores.append(make_table())
     for copy in stores:
         copy.wait()
 
@@ -344,23 +347,23 @@
         vmem = pl.BlockSpec(memory_space=pltpu.VMEM)
         hbm = pl.BlockSpec(memory_space=pl.ANY)
         dma = pltpu.SemaphoreType.DMA
-        pos, vel, means, sums = pl.pallas_call(
+        pos, vel, means, sums, live = pl.pallas_call(
             functools.partial(exchange_kernel, groups, domains, owned),
             out_shape=(
                 pltpu.VMEM((3, blocks, width), F32),
                 pltpu.VMEM((3, blocks, width), F32),
                 pltpu.VMEM((blocks, LANES), F32),
                 pltpu.VMEM((16, owned), F32),
+                pltpu.VMEM((blocks, LANES), F32),
             ),
             in_specs=[hbm] * 6 + [pl.BlockSpec(memory_space=pltpu.SMEM), hbm],
-            out_specs=(vmem, vmem, vmem, vmem),
+            out_specs=(vmem,) * 5,
             scratch_shapes=[
                 pltpu.VMEM((1, blocks), jnp.int32),
                 pltpu.VMEM((3, blocks), jnp.int32),
                 pltpu.VMEM((1, blocks), jnp.int32),
                 pltpu.VMEM((halos // LANES, LANES), jnp.int32),
                 pltpu.VMEM((blocks, width), F32),
-                pltpu.VMEM((blocks, LANES), F32),
                 pltpu.VMEM((blocks, LANES), F32),
                 pltpu.VMEM((SUMS, blocks, LANES), F32),
                 pltpu.VMEM((blocks, LANES), F32),
@@ -369,8 +372,7 @@
                 pltpu.VMEM((near, 16, blocks), F32),
                 pltpu.VMEM((far, blocks), F32),
                 dma, dma((len(chunk_spans(blocks)),)),
-                dma, dma((3,)),
-                dma, dma,
+                dma((3,)),
             ],
             compiler_params=pltpu.CompilerParams(collective_id=0, has_side_effects=True),
         )(
@@ -385,7 +387,7 @@
                 jax.ShapeDtypeStruct((blocks, width), F32),
                 jax.ShapeDtypeStruct((blocks, width), F32),
             ),
-            in_specs=[vmem, vmem, vmem, vmem],
+            in_specs=[vmem] * 5,
             out_specs=(hbm, hbm, hbm),
             scratch_shapes=[
                 pltpu.VMEM((11, owned), F32),
@@ -393,7 +395,7 @@
                 pltpu.VMEM((blocks, width), F32),
                 dma,
             ],
-        )(*[pltpu.with_memory_space_constraint(x, pltpu.VMEM) for x in (pos, vel, means, sums)])
+        )(*[pltpu.with_memory_space_constraint(x, pltpu.VMEM) for x in (pos, vel, means, sums, live)])
 
     return jax.shard_map(
         local,

time: 13.3 us -> 13.2 us (level)
  no operation moved by 1% of the time
where the time goes in v4:
time: 13.2 us; the launch traced here: 13 us
  Pallas kernels  11.7 us (89%)
  between operations  1.29 us (10%)
    pallas_call x1, Pallas kernels, local(): pl.pallas_call(functools.partial(exchange_kernel, groups, domains, owned)...  10.8 us
    pallas_call x1, Pallas kernels, local(): pl.pallas_call(functools.partial(output_kernel, halos), out_shape=(jax.Sh...  0.97 us

profile of v4, /device:TPU:0, one launch (start us, length us, event | category | flops | bytes accessed | tf_op | source)
XLA Modules:
  0.0 13.0 jit_solution(3876671824156255002)
XLA Ops:
  1.3 10.8 %shard_map.103 = (f32[3,128,512]{2,1,0:T(8,128)S(1)}, f32[3,128,512]{2,1,0:T(8,128)S(1)}, f32[128,128]{1,0:T(8,128)S(1)}, f32[16,128]{1,0:T(8,128)S(1)}, f32[128,128]{1,0:T(8,128)S(1)}) custom-call(f32[3,128,512]{2,1,0:T(8,128)} %pos_hbm.1, f32[3,128,512]{2,1,0:T(8,128)} %vel_hbm.1, f32[128,512]{1,0:T(8,128)} %mass_hbm.1, s32[1,128]{1,0:T(1,128)} %bitcast.4, ...), custom_call_target="tpu_custom_call" | custom-call | tf_op jit(solution)/shard_map/pallas_call | solution.py:350
  12.1 1.0 %shard_map.104 = (f32[11,128]{1,0:T(8,128)}, f32[128,512]{1,0:T(8,128)}, f32[128,512]{1,0:T(8,128)}) custom-call(f32[3,128,512]{2,1,0:T(8,128)S(1)} %get-tuple-element.8.pos, f32[3,128,512]{2,1,0:T(8,128)S(1)} %get-tuple-element.9.vel, f32[128,128]{1,0:T(8,128)S(1)} %get-tuple-element.10.means_ref, f32[16,128]{1,0:T(8,128)S(1)} %get-tuple-element.11.sums_ref, ...), custom_call_target="tpu_custom_call" | custom-call | tf_op jit(solution)/shard_map/pallas_call | solution.py:383

commit v5 on v4

--- a/solution.py
+++ b/solution.py
@@ -48,7 +48,7 @@
     pos_hbm, vel_hbm, mass_hbm, halo_hbm, shift_hbm, live_hbm, count_ref, home_hbm,
     pos, vel, means_ref, sums_ref, cols,
     halo_ref, shift_ref, live_ref, home_ref, mass, slots, partial, moments, tile, mass_row, near_in, far_in,
-    small_sem, in_sem, recv_sem,
+    recv_sem, small_sem=None, in_sem=None,
 ):
     blocks, width = mass.shape
     spans = chunk_spans(blocks)
@@ -265,6 +265,16 @@
     sums_ref[8:16] = jnp.where(row8 == MASS_ROW - 8, total, sums[8:16])
 
 
+def scoped_exchange(groups, domains, owned, chunks, *refs):
+    dma = pltpu.SemaphoreType.DMA
+    pl.run_scoped(
+        lambda small_sem, in_sem: exchange_kernel(
+            groups, domains, owned, *refs, small_sem=small_sem, in_sem=in_sem
+        ),
+        dma, dma((chunks,)),
+    )
+
+
 def halo_means(sums):
     scaled = sums[1:8] * (1.0 / jnp.maximum(sums[0:1], 1.0))
     centre = [scaled[k:k + 1] for k in range(3)]
@@ -274,7 +284,7 @@
 
 
 def output_kernel(
-    halos, pos, vel, means_ref, sums_ref, live_ref, table_hbm, kin_hbm, rad_hbm, table, kin, rad, sem
+    halos, pos, vel, means_ref, sums_ref, live_ref, table_hbm, kin_hbm, rad_hbm, table, kin, rad, sem=None
 ):
     blocks, width = kin.shape
     rows = blocks // CHUNKS
@@ -333,6 +343,12 @@
         copy.wait()
 
 
+def scoped_output(halos, *refs):
+    pl.run_scoped(
+        lambda sem: output_kernel(halos, *refs, sem=sem), pltpu.SemaphoreType.DMA
+    )
+
+
 def solution(mesh):
     groups, domains = mesh.shape["grp"], mesh.shape["dom"]
 
@@ -348,7 +364,7 @@
         hbm = pl.BlockSpec(memory_space=pl.ANY)
         dma = pltpu.SemaphoreType.DMA
         pos, vel, means, sums, live = pl.pallas_call(
-            functools.partial(exchange_kernel, groups, domains, owned),
+            functools.partial(scoped_exchange, groups, domains, owned, len(chunk_spans(blocks))),
             out_shape=(
                 pltpu.VMEM((3, blocks, width), F32),
                 pltpu.VMEM((3, blocks, width), F32),
@@ -371,7 +387,6 @@
                 pltpu.VMEM((1, 1, blocks), F32),
                 pltpu.VMEM((near, 16, blocks), F32),
                 pltpu.VMEM((far, blocks), F32),
-                dma, dma((len(chunk_spans(blocks)),)),
                 dma((3,)),
             ],
             compiler_params=pltpu.CompilerParams(collective_id=0, has_side_effects=True),
@@ -381,7 +396,7 @@
             block_count, home_slot.reshape(halos // LANES, LANES),
         )
         return pl.pallas_call(
-            functools.partial(output_kernel, halos),
+            functools.partial(scoped_output, halos),
             out_shape=(
                 jax.ShapeDtypeStruct((11, owned), F32),
                 jax.ShapeDtypeStruct((blocks, width), F32),
@@ -393,7 +408,6 @@
                 pltpu.VMEM((11, owned), F32),
                 pltpu.VMEM((blocks, width), F32),
                 pltpu.VMEM((blocks, width), F32),
-                dma,
             ],
         )(*[pltpu.with_memory_space_constraint(x, pltpu.VMEM) for x in (pos, vel, means, sums, live)])
 

time: 13.2 us -> 13.1 us (level)
  no operation moved by 1% of the time
where the time goes in v5:
time: 13.1 us; the launch traced here: 13 us
  Pallas kernels  11.7 us (89%)
  between operations  1.29 us (10%)
    pallas_call x1, Pallas kernels, local(): pl.pallas_call(functools.partial(scoped_exchange, groups, domains, owned,...  10.7 us
    pallas_call x1, Pallas kernels, local(): pl.pallas_call(functools.partial(scoped_output, halos), out_shape=(jax.Sh...  0.96 us

profile of v5, /device:TPU:0, one launch (start us, length us, event | category | flops | bytes accessed | tf_op | source)
XLA Modules:
  0.0 13.0 jit_solution(6003110995822260809)
XLA Ops:
  1.3 10.7 %shard_map.103 = (f32[3,128,512]{2,1,0:T(8,128)S(1)}, f32[3,128,512]{2,1,0:T(8,128)S(1)}, f32[128,128]{1,0:T(8,128)S(1)}, f32[16,128]{1,0:T(8,128)S(1)}, f32[128,128]{1,0:T(8,128)S(1)}) custom-call(f32[3,128,512]{2,1,0:T(8,128)} %refs_0_.1, f32[3,128,512]{2,1,0:T(8,128)} %refs_1_.1, f32[128,512]{1,0:T(8,128)} %refs_2_.1, s32[1,128]{1,0:T(1,128)} %bitcast.4, ...), custom_call_target="tpu_custom_call" | custom-call | tf_op jit(solution)/shard_map/pallas_call | solution.py:366
  12.0 1.0 %shard_map.104 = (f32[11,128]{1,0:T(8,128)}, f32[128,512]{1,0:T(8,128)}, f32[128,512]{1,0:T(8,128)}) custom-call(f32[3,128,512]{2,1,0:T(8,128)S(1)} %get-tuple-element.8.refs_0_, f32[3,128,512]{2,1,0:T(8,128)S(1)} %get-tuple-element.9.refs_1_, f32[128,128]{1,0:T(8,128)S(1)} %get-tuple-element.10.refs_2_, f32[16,128]{1,0:T(8,128)S(1)} %get-tuple-element.11.refs_3_, ...), custom_call_target="tpu_custom_call" | custom-call | tf_op jit(solution)/shard_map/pallas_call | solution.py:398

commit v6 on v5

--- a/solution.py
+++ b/solution.py
@@ -48,7 +48,7 @@
     pos_hbm, vel_hbm, mass_hbm, halo_hbm, shift_hbm, live_hbm, count_ref, home_hbm,
     pos, vel, means_ref, sums_ref, cols,
     halo_ref, shift_ref, live_ref, home_ref, mass, slots, partial, moments, tile, mass_row, near_in, far_in,
-    recv_sem, small_sem=None, in_sem=None,
+    recv_sem, small_sem=None, in_sem=None, tick=None,
 ):
     blocks, width = mass.shape
     spans = chunk_spans(blocks)
@@ -78,8 +78,7 @@
     near = ahead + behind + inside
     barrier = pltpu.get_barrier_semaphore()
     peers = near + far
-    for dg, dd in peers[:1]:
-        pl.semaphore_signal(barrier, inc=1, device_id=peer(dg, dd), device_id_type=MESH)
+    pl.semaphore_signal(tick, 1)
     loads = []
     for c, (start, rows) in enumerate(spans):
         part = pl.ds(start, rows)
@@ -92,8 +91,9 @@
             copy.start(priority=1)
         loads.append(group)
 
-    for dg, dd in peers[1:]:
+    for dg, dd in peers:
         pl.semaphore_signal(barrier, inc=1, device_id=peer(dg, dd), device_id_type=MESH)
+    pl.semaphore_wait(tick, 1)
 
     for copy in smalls:
         copy.wait()
@@ -203,23 +203,22 @@
     base = ((g * domains + d) * owned).astype(F32)
     mine = lax.broadcasted_iota(jnp.int32, (owned, blocks), 0).astype(F32) + base
 
-    def gather(tiles, own):
-        left, right = [], []
-        for upper, lower in tiles:
-            place = lower[0:1]
-            hit = (slots[...] == place).astype(F32)
-            if own:
-                body = jnp.concatenate([upper, jnp.where(row8 < USED_ROWS - 8, lower, 0.0)], axis=0)
-                hit = jnp.concatenate([hit, (mine == place).astype(F32)], axis=0)
-                left.append(jnp.concatenate(pieces(body), axis=0))
-            else:
-                left.append(jnp.concatenate(list(pieces(upper)) + [jnp.zeros_like(upper)], axis=0))
-            right.append(hit)
-        left = jnp.concatenate(left, axis=1).astype(BF16)
-        right = jnp.concatenate(right, axis=1).astype(BF16)
+    def matched(rows, hits):
+        left = jnp.concatenate(
+            [jnp.concatenate(list(pieces(x)), axis=0) for x in rows], axis=1
+        ).astype(BF16)
+        right = jnp.concatenate([x.astype(F32) for x in hits], axis=1).astype(BF16)
         out = lax.dot_general(left, right, (((1,), (1,)), ((), ())), preferred_element_type=F32)
-        n = 16 if own else 8
+        n = rows[0].shape[0]
         return out[0:n] + out[n:2 * n] + out[2 * n:3 * n]
+
+    def means_from(tiles):
+        return matched([t[0] for t in tiles], [slots[...] == t[1][0:1] for t in tiles])
+
+    def sums_from(tiles):
+        kept = [jnp.where(row8 < USED_ROWS - 8, t[1], 0.0) for t in tiles]
+        both = [jnp.concatenate([t[0], x], axis=0) for t, x in zip(tiles, kept)]
+        return matched(both, [mine == t[1][0:1] for t in tiles])
 
     def landed(ref, recv):
         remote(ref, ref, send, recv, *near[0]).wait_recv()
@@ -236,11 +235,11 @@
         landed(far_in, recv_far)
     tiles = inbox(from_inside)
     total = first[0:1] + masses_of(tiles)
-    held = gather([(first, second)] + tiles, True)
-    means, sums = held[0:8, :blocks], held[:, blocks:]
+    means = means_from([(first, second)] + tiles)
+    sums = sums_from([(first, second)] + tiles)
     tiles = inbox(from_ahead)
     total = total + masses_of(tiles)
-    means = means + gather(tiles, False)
+    means = means + means_from(tiles)
     whole = near_in.at[:, used]
     remote(whole, whole, send, early, *near[0]).wait_send()
     if far:
@@ -249,9 +248,7 @@
     landed(near_in.at[pl.ds(0, domains), used], late)
     tiles = inbox(from_behind)
     total = total + masses_of(tiles)
-    held = gather(tiles, True)
-    means = means + held[0:8, :blocks]
-    sums = sums + held[:, blocks:]
+    means = means + means_from(tiles)
 
     centre, drift, spread = halo_means(means)
     by_block = jnp.concatenate(
@@ -261,6 +258,7 @@
         axis=0,
     )
     means_ref[:, 0:8] = by_block.T
+    sums = sums + sums_from(tiles)
     sums_ref[0:8] = sums[0:8]
     sums_ref[8:16] = jnp.where(row8 == MASS_ROW - 8, total, sums[8:16])
 
@@ -268,10 +266,10 @@
 def scoped_exchange(groups, domains, owned, chunks, *refs):
     dma = pltpu.SemaphoreType.DMA
     pl.run_scoped(
-        lambda small_sem, in_sem: exchange_kernel(
-            groups, domains, owned, *refs, small_sem=small_sem, in_sem=in_sem
+        lambda small_sem, in_sem, tick: exchange_kernel(
+            groups, domains, owned, *refs, small_sem=small_sem, in_sem=in_sem, tick=tick
         ),
-        dma, dma((chunks,)),
+        dma, dma((chunks,)), pltpu.SemaphoreType.REGULAR,
     )
 
 

time: 13.1 us -> 13.1 us (level)
  no operation moved by 1% of the time
where the time goes in v6:
time: 13.1 us; the launch traced here: 13 us
  Pallas kernels  11.7 us (89%)
  between operations  1.29 us (10%)
    pallas_call x1, Pallas kernels, local(): pl.pallas_call(functools.partial(scoped_exchange, groups, domains, owned,...  10.7 us
    pallas_call x1, Pallas kernels, local(): pl.pallas_call(functools.partial(scoped_output, halos), out_shape=(jax.Sh...  0.96 us

profile of v6, /device:TPU:0, one launch (start us, length us, event | category | flops | bytes accessed | tf_op | source)
XLA Modules:
  0.0 13.0 jit_solution(4855635083178526599)
XLA Ops:
  1.3 10.7 %shard_map.103 = (f32[3,128,512]{2,1,0:T(8,128)S(1)}, f32[3,128,512]{2,1,0:T(8,128)S(1)}, f32[128,128]{1,0:T(8,128)S(1)}, f32[16,128]{1,0:T(8,128)S(1)}, f32[128,128]{1,0:T(8,128)S(1)}) custom-call(f32[3,128,512]{2,1,0:T(8,128)} %refs_0_.1, f32[3,128,512]{2,1,0:T(8,128)} %refs_1_.1, f32[128,512]{1,0:T(8,128)} %refs_2_.1, s32[1,128]{1,0:T(1,128)} %bitcast.4, ...), custom_call_target="tpu_custom_call" | custom-call | tf_op jit(solution)/shard_map/pallas_call | solution.py:364
  12.0 1.0 %shard_map.104 = (f32[11,128]{1,0:T(8,128)}, f32[128,512]{1,0:T(8,128)}, f32[128,512]{1,0:T(8,128)}) custom-call(f32[3,128,512]{2,1,0:T(8,128)S(1)} %get-tuple-element.8.refs_0_, f32[3,128,512]{2,1,0:T(8,128)S(1)} %get-tuple-element.9.refs_1_, f32[128,128]{1,0:T(8,128)S(1)} %get-tuple-element.10.refs_2_, f32[16,128]{1,0:T(8,128)S(1)} %get-tuple-element.11.refs_3_, ...), custom_call_target="tpu_custom_call" | custom-call | tf_op jit(solution)/shard_map/pallas_call | solution.py:396
